TPU v7x, 32 devices: a whole 2x2x4 slice. The times are simulated.
32 devices in a mesh: ctx: 8 (over z, y), wt: 4 (over x, core).
Axes of the slice: x: 2, y: 2, z: 4, core: 2. Of those that a mesh axis runs over, the one named last changes fastest.
Arguments:
- tokens: bfloat16 [4, 2048, 2048], P('wt', 'ctx'), may hold values from -6 to 6
- out_grad: bfloat16 [4, 2048, 2048], P('wt', 'ctx'), may hold values from -6 to 6
- segments: int32 [4, 2048], P('wt', 'ctx'), may hold values from 0 to 7, never falling along the last dimension, each value on 1 to 1024 neighbouring positions
- adapter_index: int32 [4], P('wt'), may hold values from 0 to 7
- first_gain: float32 [2048], replicated, may hold values from 0.1 to 1.9
- first_bias: float32 [2048], replicated, may hold values from -3 to 3
- second_gain: float32 [2048], replicated, may hold values from 0.1 to 1.9
- second_bias: float32 [2048], replicated, may hold values from -3 to 3
- qkv_weight: bfloat16 [2048, 2304], P('wt'), may hold values from -0.125 to 0.125
- out_weight: bfloat16 [2048, 2048], P('wt'), may hold values from -0.5 to 0.5
- expand_weight: bfloat16 [2048, 8192], P('wt'), may hold values from -0.125 to 0.125
- shrink_weight: bfloat16 [8192, 2048], P('wt'), may hold values from -0.0625 to 0.0625
- query_first: bfloat16 [8, 2048, 16], replicated, may hold values from -0.125 to 0.125
- query_second: bfloat16 [8, 16, 2048], replicated, may hold values from -1.5 to 1.5
- key_first: bfloat16 [8, 2048, 16], replicated, may hold values from -0.125 to 0.125
- key_second: bfloat16 [8, 16, 128], replicated, may hold values from -1.5 to 1.5
- value_first: bfloat16 [8, 2048, 16], replicated, may hold values from -0.125 to 0.125
- value_second: bfloat16 [8, 16, 128], replicated, may hold values from -1.5 to 1.5
- output_first: bfloat16 [8, 2048, 16], replicated, may hold values from -0.5 to 0.5
- output_second: bfloat16 [8, 16, 2048], replicated, may hold values from -1.5 to 1.5
- expand_first: bfloat16 [8, 2048, 16], replicated, may hold values from -0.125 to 0.125
- expand_second: bfloat16 [8, 16, 8192], replicated, may hold values from -1.5 to 1.5
- shrink_first: bfloat16 [8, 8192, 16], replicated, may hold values from -0.0625 to 0.0625
- shrink_second: bfloat16 [8, 16, 2048], replicated, may hold values from -1.5 to 1.5
Outputs:
- layer_out: bfloat16 [4, 2048, 2048], P('wt', 'ctx')
- tokens_grad: bfloat16 [4, 2048, 2048], P('wt', 'ctx')
- grad_query_first: float32 [8, 2048, 16], P(None, 'wt')
- grad_query_second: float32 [8, 16, 2048], P(None, None, 'wt')
- grad_key_first: float32 [8, 2048, 16], P(None, 'wt')
- grad_key_second: float32 [8, 16, 128], P(None, None, 'wt')
- grad_value_first: float32 [8, 2048, 16], P(None, 'wt')
- grad_value_second: float32 [8, 16, 128], P(None, None, 'wt')
- grad_output_first: float32 [8, 2048, 16], P(None, 'wt')
- grad_output_second: float32 [8, 16, 2048], P(None, None, 'wt')
- grad_expand_first: float32 [8, 2048, 16], P(None, 'wt')
- grad_expand_second: float32 [8, 16, 8192], P(None, None, 'wt')
- grad_shrink_first: float32 [8, 8192, 16], P(None, 'wt')
- grad_shrink_second: float32 [8, 16, 2048], P(None, None, 'wt')
Inputs may be any that keep to these rules, and one draw needn't show every extreme that they name: `segments`: within each sequence the numbers never fall; a document is a run of equal numbers of at most 1024 positions.
All inputs are finite; a program needn't handle non-finite values.
Results may differ from a plain program's by a relative error of at most 0.02.
Values may be sent and summed in bfloat16 or wider, within the bound.
A program may use at most 320 MiB of HBM per device.

v0:
```python
import math
import jax
import jax.numpy as jnp
from jax import lax
from jax.sharding import PartitionSpec as P

HEADS = 16
HEAD = 128
ADAPTERS = 8
KEY_BLOCK = 512
EPSILON = 1e-05
LOWEST = -1e30


def matmul(left, right):
    return jnp.dot(left, right, preferred_element_type=jnp.float32)


def matmul_right_t(left, right):
    return lax.dot_general(
        left, right, (((1,), (1,)), ((), ())), preferred_element_type=jnp.float32
    )


def matmul_left_t(left, right):
    return lax.dot_general(
        left, right, (((0,), (0,)), ((), ())), preferred_element_type=jnp.float32
    )


def layer_norm(values, gain, offset):
    centre = values - jnp.mean(values, -1, keepdims=True)
    scale_inv = lax.rsqrt(jnp.mean(centre * centre, -1, keepdims=True) + EPSILON)
    normed = centre * scale_inv
    return (normed * gain + offset, normed, scale_inv)


def norm_back(grad_out, gain, normed, scale_inv):
    grad_norm = grad_out * gain
    return scale_inv * (
        grad_norm
        - jnp.mean(grad_norm, -1, keepdims=True)
        - normed * jnp.mean(grad_norm * normed, -1, keepdims=True)
    )


def gelu_tanh(values):
    return jax.nn.gelu(values, approximate=True)


def fold_rows(left, piece):
    return matmul(left, piece)


def project_back(grad_low, piece):
    return matmul_right_t(grad_low, piece)


def spread_table(onehot, table):
    return onehot[:, None, None] * table[None]


def body(
    tokens,
    out_grad,
    segments,
    adapter_index,
    first_gain,
    first_bias,
    second_gain,
    second_bias,
    qkv_weight,
    out_weight,
    expand_weight,
    shrink_weight,
    query_first,
    query_second,
    key_first,
    key_second,
    value_first,
    value_second,
    output_first,
    output_second,
    expand_first,
    expand_second,
    shrink_first,
    shrink_second,
):
    hidden = tokens[0].astype(jnp.float32)
    tok_count = hidden.shape[0]
    model_width = hidden.shape[1]
    chosen = adapter_index[0]

    def select(table):
        return lax.dynamic_index_in_dim(table, chosen, 0, keepdims=False)

    own_query_first = select(query_first)
    own_query_second = select(query_second)
    own_key_first = select(key_first)
    own_key_second = select(key_second)
    own_value_first = select(value_first)
    own_value_second = select(value_second)
    own_output_first = select(output_first)
    own_output_second = select(output_second)
    own_expand_first = select(expand_first)
    own_expand_second = select(expand_second)
    own_shrink_first = select(shrink_first)
    own_shrink_second = select(shrink_second)
    rank_width = own_query_first.shape[1]
    score_scale = 1.0 / math.sqrt(HEAD)
    normed_one, plain_one, inverse_one = layer_norm(hidden, first_gain, first_bias)
    first_low = normed_one.astype(jnp.bfloat16)
    attn_first = jnp.concatenate([own_query_first, own_key_first, own_value_first], 1)
    low_rank = matmul(first_low, attn_first).astype(jnp.bfloat16)
    base = fold_rows(first_low, lax.all_gather(qkv_weight, "wt", axis=0, tiled=True))
    query = (
        (base[:, :model_width] + matmul(low_rank[:, :rank_width], own_query_second))
        .astype(jnp.bfloat16)
        .reshape(tok_count, HEADS, HEAD)
    )
    keys_own = (
        base[:, model_width : model_width + HEAD]
        + matmul(low_rank[:, rank_width : 2 * rank_width], own_key_second)
    ).astype(jnp.bfloat16)
    values_own = (
        base[:, model_width + HEAD :] + matmul(low_rank[:, 2 * rank_width :], own_value_second)
    ).astype(jnp.bfloat16)
    keys_all, values_all, segs_all = (
        lax.all_gather(keys_own, "ctx", axis=0, tiled=True),
        lax.all_gather(values_own, "ctx", axis=0, tiled=True),
        lax.all_gather(segments[0], "ctx", axis=0, tiled=True),
    )
    query_segs = segments[0]
    position = lax.axis_index("ctx") * tok_count + jnp.arange(tok_count, dtype=jnp.int32)
    first_block = jnp.sum((segs_all < query_segs[0]).astype(jnp.int32)) // KEY_BLOCK
    stop_block = position[tok_count - 1] // KEY_BLOCK + 1
    offsets = jnp.arange(KEY_BLOCK, dtype=jnp.int32)

    def block_scores(start):
        key_block = lax.dynamic_slice_in_dim(keys_all, start, KEY_BLOCK, 0)
        value_block = lax.dynamic_slice_in_dim(values_all, start, KEY_BLOCK, 0)
        seg_block = lax.dynamic_slice_in_dim(segs_all, start, KEY_BLOCK, 0)
        allowed = (query_segs[:, None] == seg_block[None, :]) & (
            position[:, None] >= start + offsets[None, :]
        )
        raw = (
            jnp.einsum("thd,kd->thk", query, key_block, preferred_element_type=jnp.float32)
            * score_scale
        )
        return (jnp.where(allowed[:, None, :], raw, LOWEST), allowed, key_block, value_block)

    def stats_step(index, carry):
        highest, total = carry
        scores, allowed, key_block, value_block = block_scores(index * KEY_BLOCK)
        new_high = jnp.maximum(highest, jnp.max(scores, -1))
        weights = jnp.where(allowed[:, None, :], jnp.exp(scores - new_high[..., None]), 0.0)
        return (new_high, total * jnp.exp(highest - new_high) + jnp.sum(weights, -1))

    highest, total = lax.fori_loop(
        first_block,
        stop_block,
        stats_step,
        (
            jnp.full((tok_count, HEADS), LOWEST, jnp.float32),
            jnp.zeros((tok_count, HEADS), jnp.float32),
        ),
    )
    log_total = highest + jnp.log(total)

    def value_step(index, gathered):
        scores, allowed, key_block, value_block = block_scores(index * KEY_BLOCK)
        probs = jnp.where(allowed[:, None, :], jnp.exp(scores - log_total[..., None]), 0.0).astype(
            jnp.bfloat16
        )
        return gathered + jnp.einsum(
            "thk,kd->thd", probs, value_block, preferred_element_type=jnp.float32
        )

    attended = lax.fori_loop(
        first_block, stop_block, value_step, jnp.zeros((tok_count, HEADS, HEAD), jnp.float32)
    )
    attended_low = attended.reshape(tok_count, model_width).astype(jnp.bfloat16)
    output_low = matmul(attended_low, own_output_first).astype(jnp.bfloat16)
    branch = fold_rows(attended_low, lax.all_gather(out_weight, "wt", axis=0, tiled=True))
    middle = hidden + branch + matmul(output_low, own_output_second)
    normed_two, plain_two, inverse_two = layer_norm(middle, second_gain, second_bias)
    second_low = normed_two.astype(jnp.bfloat16)
    expand_low = matmul(second_low, own_expand_first).astype(jnp.bfloat16)
    upward = fold_rows(
        second_low, lax.all_gather(expand_weight, "wt", axis=0, tiled=True)
    ) + matmul(expand_low, own_expand_second)
    active, gelu_pull = jax.vjp(gelu_tanh, upward)
    active_low = active.astype(jnp.bfloat16)
    shrink_low = matmul(active_low, own_shrink_first).astype(jnp.bfloat16)
    shrunk = fold_rows(active_low, lax.all_gather(shrink_weight, "wt", axis=0, tiled=True))
    layer_out = (middle + shrunk + matmul(shrink_low, own_shrink_second)).astype(jnp.bfloat16)[None]
    grad_low = out_grad[0]
    grad_top = grad_low.astype(jnp.float32)
    grad_shrink_low = matmul_right_t(grad_low, own_shrink_second).astype(jnp.bfloat16)
    grad_active = project_back(
        grad_low, lax.all_gather(shrink_weight, "wt", axis=0, tiled=True)
    ) + matmul_right_t(grad_shrink_low, own_shrink_first)
    shrink_second_grad = matmul_left_t(shrink_low, grad_low)
    shrink_first_grad = matmul_left_t(active_low, grad_shrink_low)
    grad_active_low = grad_active.astype(jnp.bfloat16)
    grad_upward = gelu_pull(grad_active_low.astype(jnp.float32))[0].astype(jnp.bfloat16)
    grad_expand_low = matmul_right_t(grad_upward, own_expand_second).astype(jnp.bfloat16)
    grad_second = project_back(
        grad_upward, lax.all_gather(expand_weight, "wt", axis=0, tiled=True)
    ) + matmul_right_t(grad_expand_low, own_expand_first)
    expand_second_grad = matmul_left_t(expand_low, grad_upward)
    expand_first_grad = matmul_left_t(second_low, grad_expand_low)
    grad_middle = grad_top + norm_back(grad_second, second_gain, plain_two, inverse_two)
    grad_branch = grad_middle.astype(jnp.bfloat16)
    grad_output_low = matmul_right_t(grad_branch, own_output_second).astype(jnp.bfloat16)
    grad_attended = project_back(
        grad_branch, lax.all_gather(out_weight, "wt", axis=0, tiled=True)
    ) + matmul_right_t(grad_output_low, own_output_first)
    output_second_grad = matmul_left_t(output_low, grad_branch)
    output_first_grad = matmul_left_t(attended_low, grad_output_low)
    grad_attn_low = grad_attended.astype(jnp.bfloat16).reshape(tok_count, HEADS, HEAD)
    delta = jnp.sum(grad_attn_low.astype(jnp.float32) * attended, -1)
    seq_length = keys_all.shape[0]

    def back_step(index, carry):
        grad_query, grad_keys, grad_values = carry
        start = index * KEY_BLOCK
        scores, allowed, key_block, value_block = block_scores(start)
        probs = jnp.where(allowed[:, None, :], jnp.exp(scores - log_total[..., None]), 0.0)
        probs_low = probs.astype(jnp.bfloat16)
        grad_probs = jnp.einsum(
            "thd,kd->thk", grad_attn_low, value_block, preferred_element_type=jnp.float32
        )
        grad_scores = (probs * (grad_probs - delta[..., None])).astype(jnp.bfloat16)
        grad_query = grad_query + jnp.einsum(
            "thk,kd->thd", grad_scores, key_block, preferred_element_type=jnp.float32
        )
        key_part = jnp.einsum("thk,thd->kd", grad_scores, query, preferred_element_type=jnp.float32)
        value_part = jnp.einsum(
            "thk,thd->kd", probs_low, grad_attn_low, preferred_element_type=jnp.float32
        )
        grad_keys = lax.dynamic_update_slice_in_dim(grad_keys, key_part, start, 0)
        grad_values = lax.dynamic_update_slice_in_dim(grad_values, value_part, start, 0)
        return (grad_query, grad_keys, grad_values)

    start_carry = (
        jnp.zeros((tok_count, HEADS, HEAD), jnp.float32),
        jnp.zeros((seq_length, HEAD), jnp.float32),
        jnp.zeros((seq_length, HEAD), jnp.float32),
    )
    grad_query, grad_keys, grad_values = lax.fori_loop(
        first_block, stop_block, back_step, start_carry
    )
    own_key_grad, own_value_grad = (
        lax.psum_scatter(
            (grad_keys * score_scale).astype(jnp.bfloat16), "ctx", scatter_dimension=0, tiled=True
        ).astype(jnp.float32),
        lax.psum_scatter(
            grad_values.astype(jnp.bfloat16), "ctx", scatter_dimension=0, tiled=True
        ).astype(jnp.float32),
    )
    grad_query_low = (grad_query * score_scale).reshape(tok_count, model_width).astype(jnp.bfloat16)
    own_key_low = own_key_grad.astype(jnp.bfloat16)
    own_value_low = own_value_grad.astype(jnp.bfloat16)
    grad_qkv_low = jnp.concatenate([grad_query_low, own_key_low, own_value_low], 1)
    grad_rank = jnp.concatenate(
        [
            matmul_right_t(grad_query_low, own_query_second),
            matmul_right_t(own_key_low, own_key_second),
            matmul_right_t(own_value_low, own_value_second),
        ],
        1,
    ).astype(jnp.bfloat16)
    grad_first = project_back(
        grad_qkv_low, lax.all_gather(qkv_weight, "wt", axis=0, tiled=True)
    ) + matmul_right_t(grad_rank, attn_first)
    query_second_grad = matmul_left_t(low_rank[:, :rank_width], grad_query_low)
    key_second_grad = matmul_left_t(low_rank[:, rank_width : 2 * rank_width], own_key_low)
    value_second_grad = matmul_left_t(low_rank[:, 2 * rank_width :], own_value_low)
    attn_first_grad = matmul_left_t(first_low, grad_rank)
    query_first_grad = attn_first_grad[:, :rank_width]
    key_first_grad = attn_first_grad[:, rank_width : 2 * rank_width]
    value_first_grad = attn_first_grad[:, 2 * rank_width :]
    tokens_grad = (grad_middle + norm_back(grad_first, first_gain, plain_one, inverse_one)).astype(
        jnp.bfloat16
    )[None]
    onehot = (jnp.arange(ADAPTERS, dtype=jnp.int32) == chosen).astype(jnp.float32)
    summed = lax.psum(
        (
            spread_table(onehot, query_first_grad),
            spread_table(onehot, query_second_grad),
            spread_table(onehot, key_first_grad),
            spread_table(onehot, key_second_grad),
            spread_table(onehot, value_first_grad),
            spread_table(onehot, value_second_grad),
            spread_table(onehot, output_first_grad),
            spread_table(onehot, output_second_grad),
            spread_table(onehot, expand_first_grad),
            spread_table(onehot, expand_second_grad),
            spread_table(onehot, shrink_first_grad),
            spread_table(onehot, shrink_second_grad),
        ),
        ("ctx", "wt"),
    )
    member = lax.axis_index("wt")
    members = lax.axis_size("wt")
    shares = []
    for number, table in enumerate(summed):
        axis_dim = 1 + number % 2
        share_len = table.shape[axis_dim] // members
        shares.append(lax.dynamic_slice_in_dim(table, member * share_len, share_len, axis_dim))
    return (
        layer_out,
        tokens_grad,
        shares[0],
        shares[1],
        shares[2],
        shares[3],
        shares[4],
        shares[5],
        shares[6],
        shares[7],
        shares[8],
        shares[9],
        shares[10],
        shares[11],
    )


def solution(mesh):
    placed = (
        P("wt", "ctx", None),
        P("wt", "ctx", None),
        P("wt", "ctx"),
        P("wt"),
        P(),
        P(),
        P(),
        P(),
        P("wt", None),
        P("wt", None),
        P("wt", None),
        P("wt", None),
        P(),
        P(),
        P(),
        P(),
        P(),
        P(),
        P(),
        P(),
        P(),
        P(),
        P(),
        P(),
    )
    return jax.shard_map(
        body,
        mesh=mesh,
        in_specs=placed,
        out_specs=(
            P("wt", "ctx", None),
            P("wt", "ctx", None),
            P(None, "wt", None),
            P(None, None, "wt"),
            P(None, "wt", None),
            P(None, None, "wt"),
            P(None, "wt", None),
            P(None, None, "wt"),
            P(None, "wt", None),
            P(None, None, "wt"),
            P(None, "wt", None),
            P(None, None, "wt"),
            P(None, "wt", None),
            P(None, None, "wt"),
        ),
        check_vma=False,
    )
```

profile of v0, /device:TPU:0, one launch (start us, length us, event | category | flops | bytes accessed | tf_op | source)
XLA Modules:
  0.0 1124.4 jit_solution(9140331551840397132)
XLA Ops:
  10.6 22.3 %all-gather = s32[1,2048]{1,0:T(1,128)S(1)} all-gather(s32[1,256]{1,0:T(1,128)S(1)} %copy-done.26), channel_id=2, replica_groups=mesh['ctx'=8,'wt'=4] {'ctx'}, dimensions={1}, use_global_device_ids=true | all-gather | bytes 9216 | tf_op jit(solution)/shard_map/all_gather | solution.py:131
  44.5 1.6 convolution_convert_fusion.6
  48.1 28.4 %all-gather.6.cloned.1.call-done = bf16[2048,2304]{1,0:T(8,128)(2,1)} async-done(((bf16[512,2304]{1,0:T(8,128)(2,1)}), bf16[2048,2304]{1,0:T(8,128)(2,1)}) %all-gather.6.cloned.1.call-update) | async-done | bytes 9437200 | tf_op jit(solution)/shard_map/all_gather | solution.py:115
  76.5 6.6 fusion.188
  86.7 33.2 %all_gather.27 = bf16[2048,128]{1,0:T(8,128)(2,1)} all-gather(bf16[256,128]{1,0:T(8,128)(2,1)S(1)} %fusion.109), channel_id=1, replica_groups=mesh['ctx'=8,'wt'=4] {'ctx'}, dimensions={0}, use_global_device_ids=true | all-gather | bytes 589824 | tf_op jit(solution)/shard_map/all_gather | solution.py:129
  120.3 4.7 while.39
  120.6 2.3 fusion.266
  122.9 2.0 select_reduce_fusion.2
  126.1 37.9 %all_gather.28 = bf16[2048,128]{1,0:T(8,128)(2,1)} all-gather(bf16[256,128]{1,0:T(8,128)(2,1)S(1)} %fusion.110), channel_id=1, replica_groups=mesh['ctx'=8,'wt'=4] {'ctx'}, dimensions={0}, use_global_device_ids=true | all-gather | bytes 589824 | tf_op jit(solution)/shard_map/all_gather | solution.py:130
  164.0 1.6 broadcast.224.clone
  165.6 6.6 while.40
  165.8 6.1 fusion.271
  172.1 2.5 copy.45
  174.7 1.5 convolution_convert_fusion.4
  176.2 6.3 fusion.83
  188.0 151.6 %all-gather.10.cloned.1.call-done = bf16[2048,8192]{1,0:T(8,128)(2,1)} async-done(((bf16[512,8192]{1,0:T(8,128)(2,1)}), bf16[2048,8192]{1,0:T(8,128)(2,1)}) %all-gather.10.cloned.1.call-update) | async-done | bytes 33554448 | tf_op jit(solution)/shard_map/all_gather | solution.py:190
  339.6 22.7 %fusion.189 = f32[256,8192]{1,0:T(8,128)} fusion(bf16[256,2048]{1,0:T(8,128)(2,1)} %copy-done.17, bf16[2048,8192]{1,0:T(8,128)(2,1)} %all-gather.10.cloned.1.call-done), kind=kOutput, calls=%fused_computation.265 | convolution fusion | flops 8589934592 | bytes 42991616 | tf_op jit(solution)/shard_map/dot_general | solution.py:16
  362.2 10.3 multiply_convert_fusion
  372.6 169.9 %all-gather.12.cloned.1.call-done = bf16[8192,2048]{1,0:T(8,128)(2,1)} async-done(((bf16[2048,2048]{1,0:T(8,128)(2,1)}), bf16[8192,2048]{1,0:T(8,128)(2,1)}) %all-gather.12.cloned.1.call-update) | async-done | bytes 33554448 | tf_op jit(solution)/shard_map/all_gather | solution.py:195
  542.5 18.5 %fusion.115 = f32[256,8192]{1,0:T(8,128)} fusion(bf16[8192,2048]{1,0:T(8,128)(2,1)} %all-gather.12.cloned.1.call-done, bf16[1,256,2048]{2,1,0:T(8,128)(2,1)} %param.31), kind=kOutput, calls=%fused_computation.152 | convolution fusion | flops 8589934592 | bytes 42991616 | tf_op jit(solution)/shard_map/dot_general | solution.py:20
  561.0 24.8 %fusion.73 = bf16[256,8192]{1,0:T(8,128)(2,1)S(1)} fusion(f32[256,8192]{1,0:T(8,128)} %get-tuple-element.439, f32[256,8192]{1,0:T(8,128)} %fusion.115, bf16[16,256]{1,0:T(8,128)(2,1)S(1)} %convolution_convert_fusion.6, bf16[8,8192,16]{1,2,0:T(8,128)(2,1)} %param.52, s32[]{:T(128)S(6)} %select_n.82), kind=kOutput, calls=%fused_computation.77 | convolution fusion | flops 115343360 | bytes 21241860 | tf_op jit(solution)/shard_map/dot_general | solution.py:20
  585.9 2.1 copy-done.13
  589.1 17.0 %fusion.190 = f32[256,2048]{1,0:T(8,128)} fusion(bf16[256,8192]{1,0:T(8,128)(2,1)} %copy-done.13, bf16[2048,8192]{1,0:T(8,128)(2,1)} %all-gather.10.cloned.1.call-done), kind=kOutput, calls=%fused_computation.266 | convolution fusion | flops 8589934592 | bytes 39845888 | tf_op jit(solution)/shard_map/dot_general | solution.py:20
  606.1 2.6 fusion.185
  609.5 2.3 convolution_convert_fusion.5
  611.9 2.4 fusion.182
  618.5 1.5 fusion.192
  620.1 2.1 convolution_convert_fusion.9
  622.2 1.5 fusion.194
  625.0 15.0 %while.41 = (s32[]{:T(128)}, f32[256,16,128]{2,0,1:T(8,128)S(1)}, f32[2048,128]{0,1:T(8,128)}, bf16[2048,128]{0,1:T(8,128)(2,1)}, s32[]{:T(128)}, /*index=5*/s32...) while((s32[]{:T(128)}, f32[256,16,128]{2,0,1:T(8,128)S(1)}, ...), condition=%wide.region_15.16_spmd.clone, body=%wide.region_14.15_spmd.clone.sunk | while | flops 2710438656 | bytes 55899472 | solution.py:251
  625.0 2.2 fusion.282
  627.6 4.1 fusion.283
  631.7 2.6 convolution_add_fusion.13
  634.3 2.3 fusion.284
  636.5 2.5 fusion.285
  640.1 3.8 broadcast_multiply_fusion.1
  643.9 2.5 broadcast_multiply_fusion
  646.6 1.9 copy.49
  648.5 2.0 multiply_convert_fusion.1
  650.5 1.7 fusion.149
  653.2 1.7 convolution_convert_fusion.3
  655.2 2.8 broadcast_multiply_fusion.2
  658.0 74.1 %reduce-scatter.5.cloned.1.call-done = bf16[256,128]{0,1:T(8,128)(2,1)} async-done(((bf16[2048,128]{0,1:T(8,128)(2,1)}), bf16[256,128]{0,1:T(8,128)(2,1)}) %reduce-scatter.5.cloned.1.call-update) | async-done | bytes 65552 | tf_op jit(solution)/shard_map/reduce_scatter | solution.py:258
  733.1 65.0 %reduce-scatter.3.cloned.1.call-done = bf16[256,128]{0,1:T(8,128)(2,1)} async-done(((bf16[2048,128]{0,1:T(8,128)(2,1)}), bf16[256,128]{0,1:T(8,128)(2,1)}) %reduce-scatter.3.cloned.1.call-update) | async-done | bytes 65552 | tf_op jit(solution)/shard_map/reduce_scatter | solution.py:255
  799.1 1.5 fusion.145
  803.4 2.5 broadcast_multiply_fusion.3
  806.0 1.6 copy-done.4
  807.6 17.9 %convolution_add_fusion.9 = f32[256,2048]{1,0:T(8,128)S(1)} fusion(f32[256,2048]{1,0:T(8,128)S(1)} %copy-done.4, bf16[256,8192]{1,0:T(8,128)(2,1)} %get-tuple-element.438, bf16[8192,2048]{1,0:T(8,128)(2,1)} %all-gather.12.cloned.1.call-done), kind=kOutput, calls=%fused_computation.98 | convolution fusion | flops 8590458880 | bytes 41943040 | tf_op jit(solution)/shard_map/dot_general | solution.py:16
  825.5 2.3 fusion.93
  827.8 5.6 fusion.103
  835.2 1.7 fusion.111
  836.9 259.0 %all-reduce.3.cloned.1.call-done = (f32[8,2048,16]{1,2,0:T(8,128)}, f32[8,16,2048]{2,1,0:T(8,128)}, f32[8,2048,16]{1,2,0:T(8,128)}, f32[8,16,128]{2,1,0:T(8,128)...) async-done(((f32[8,2048,16]{1,2,0:T(8,128)}, ...) | async-done | bytes 16908304 | tf_op jit(solution)/shard_map/psum | solution.py:288
  1096.0 1.8 constant_dynamic-slice_fusion.11
  1097.8 1.7 constant_dynamic-slice_fusion.10
  1099.5 1.7 constant_dynamic-slice_fusion.9
  1101.1 1.7 constant_dynamic-slice_fusion.7
  1102.8 1.6 constant_dynamic-slice_fusion.8
  1104.4 1.6 constant_dynamic-slice_fusion.6
  1105.9 1.7 constant_dynamic-slice_fusion.5
  1107.6 1.7 constant_dynamic-slice_fusion.4
  1109.3 1.7 constant_dynamic-slice_fusion.3
  1110.9 2.3 constant_dynamic-slice_fusion.2
  1113.2 2.3 constant_dynamic-slice_fusion.1
  1115.5 1.7 constant_dynamic-slice_fusion
  (186 shorter events, 38.3 us)
Async XLA Ops:
  7.2 355.1 %copy-start = (bf16[8,16,8192]{2,1,0:T(8,128)(2,1)S(1)}, bf16[8,16,8192]{2,1,0:T(8,128)(2,1)}, u32[]{:S(2)}) copy-start(bf16[8,16,8192]{2,1,0:T(8,128)(2,1)} %param.51) | copy-start | bytes 6291460
  7.2 69.3 %all-gather.6.cloned.1.call-start = ((), (), s32[]{:S(2)}) async-start(), calls=%async_computation.2 | async-start | bytes 11796480 | tf_op jit(solution)/shard_map/all_gather | solution.py:115
  7.9 168.3 %all-gather.8.cloned.1.call-start = ((), (), s32[]{:S(2)}) async-start(), calls=%async_computation.3 | async-start | bytes 10485760 | tf_op jit(solution)/shard_map/all_gather | solution.py:184
  8.7 330.9 %all-gather.10.cloned.1.call-start = ((), (), s32[]{:S(2)}) async-start(), calls=%async_computation.4 | async-start | bytes 41943040 | tf_op jit(solution)/shard_map/all_gather | solution.py:190
  9.4 0.7 copy-start.26
  9.4 31.8 %copy-start.5 = (bf16[1,256,2048]{2,1,0:T(8,128)(2,1)S(1)}, bf16[1,256,2048]{2,1,0:T(8,128)(2,1)}, u32[]{:S(2)}) copy-start(bf16[1,256,2048]{2,1,0:T(8,128)(2,1)} %param.30) | copy-start | bytes 3145732
  9.4 533.1 %all-gather.12.cloned.1.call-start = ((), (), s32[]{:S(2)}) async-start(), calls=%async_computation.5 | async-start | bytes 41943040 | tf_op jit(solution)/shard_map/all_gather | solution.py:195
  10.0 36.2 %copy-start.41 = (f32[2048]{0:T(1024)S(1)}, f32[2048]{0:T(1024)}, u32[]{:S(2)}) copy-start(f32[2048]{0:T(1024)} %param.34) | copy-start | bytes 24580
  10.0 36.2 %copy-start.49 = (f32[2048]{0:T(1024)S(1)}, f32[2048]{0:T(1024)}, u32[]{:S(2)}) copy-start(f32[2048]{0:T(1024)} %param.35) | copy-start | bytes 24580
  10.0 722.1 %reduce-scatter.5.cloned.1.call-start = ((), (), s32[]{:S(2)}) async-start(), calls=%async_computation.7 | async-start | bytes 589824 | tf_op jit(solution)/shard_map/reduce_scatter | solution.py:258
  41.5 5.2 copy-start.43
  41.9 4.8 copy-start.45
  42.8 40.4 %copy-start.27 = (bf16[2048,16]{0,1:T(8,128)(2,1)}, bf16[2048,16]{0,1:T(8,128)(2,1)S(1)}, u32[]{:S(2)}) copy-start(bf16[2048,16]{0,1:T(8,128)(2,1)S(1)} %dynamic-slice_bitcast_fusion.2) | copy-start | bytes 196612
  43.7 39.5 %copy-start.29 = (bf16[2048,16]{0,1:T(8,128)(2,1)}, bf16[2048,16]{0,1:T(8,128)(2,1)S(1)}, u32[]{:S(2)}) copy-start(bf16[2048,16]{0,1:T(8,128)(2,1)S(1)} %get-tuple-element.442) | copy-start | bytes 196612
  43.7 39.5 %copy-start.31 = (bf16[2048,16]{0,1:T(8,128)(2,1)}, bf16[2048,16]{0,1:T(8,128)(2,1)S(1)}, u32[]{:S(2)}) copy-start(bf16[2048,16]{0,1:T(8,128)(2,1)S(1)} %get-tuple-element.443) | copy-start | bytes 196612
  46.7 1.0 copy-start.19
  48.1 76.9 %copy-start.35 = (bf16[256,48]{0,1:T(8,128)(2,1)}, bf16[256,48]{0,1:T(8,128)(2,1)S(1)}, u32[]{:S(2)}) copy-start(bf16[256,48]{0,1:T(8,128)(2,1)S(1)} %convolution_convert_fusion) | copy-start | bytes 73732
  83.2 37.0 %copy-start.21 = (f32[256,2304]{1,0:T(8,128)}, f32[256,2304]{1,0:T(8,128)S(1)}, u32[]{:S(2)}) copy-start(f32[256,2304]{1,0:T(8,128)S(1)} %fusion.188) | copy-start | bytes 7077892
  176.2 6.3 copy-start.37
  182.5 2.8 copy-start.40
  182.6 2.7 copy-start.50
  184.0 1.3 copy-start.2
  185.8 1.0 copy-start.17
  585.8 2.1 copy-start.13
  589.1 17.0 %copy-start.3 = (f32[256,2048]{1,0:T(8,128)S(1)}, f32[256,2048]{1,0:T(8,128)}, u32[]{:S(2)}) copy-start(f32[256,2048]{1,0:T(8,128)} %copy-done.2) | copy-start | bytes 6291460
  606.1 2.6 copy-start.15
  606.1 5.7 slice-start
  608.7 3.1 slice-start.1
  609.5 4.7 copy-start.7
  614.3 2.7 copy-start.11
  614.3 3.4 copy-start.18
  614.3 3.7 copy-start.10
  615.8 2.8 copy-start.14
  617.7 2.4 copy-start.12
  625.0 15.1 %copy-start.47 = (f32[8]{0:T(128)S(1)}, f32[8]{0:T(128)}, u32[]{:S(2)}) copy-start(f32[8]{0:T(128)} %compare_convert_fusion) | copy-start | bytes 100
  625.0 2.6 copy-start.25
  634.2 2.3 copy-start.23
  639.0 0.8 copy-start.24
  640.0 6.3 copy-start.16
  640.1 158.1 %reduce-scatter.3.cloned.1.call-start = ((), (), s32[]{:S(2)}) async-start(), calls=%async_computation.6 | async-start | bytes 589824 | tf_op jit(solution)/shard_map/reduce_scatter | solution.py:255
  640.1 3.8 copy-start.22
  648.5 3.7 copy-start.20
  648.5 6.4 copy-start.8
  648.5 6.4 copy-start.38
  653.2 442.8 %all-reduce.3.cloned.1.call-start = ((), (), s32[]{:S(2)}) async-start(), calls=%async_computation.8 | async-start | bytes 33816576 | tf_op jit(solution)/shard_map/psum | solution.py:288
  655.2 145.5 %copy-start.36 = (bf16[256,48]{0,1:T(8,128)(2,1)S(1)}, bf16[256,48]{0,1:T(8,128)(2,1)}, u32[]{:S(2)}) copy-start(bf16[256,48]{0,1:T(8,128)(2,1)} %copy-done.35) | copy-start | bytes 73732
  655.2 147.5 %copy-start.48 = (f32[8]{0:T(128)S(1)}, f32[8]{0:T(128)}, u32[]{:S(2)}) copy-start(f32[8]{0:T(128)} %compare_convert_fusion) | copy-start | bytes 100
  806.0 1.6 copy-start.4
  807.6 20.2 %copy-start.33 = (bf16[256,128]{0,1:T(8,128)(2,1)S(1)}, bf16[256,128]{0,1:T(8,128)(2,1)}, u32[]{:S(2)}) copy-start(bf16[256,128]{0,1:T(8,128)(2,1)} %reduce-scatter.5.cloned.1.call-done) | copy-start | bytes 196612
  807.6 20.2 %copy-start.34 = (bf16[256,128]{0,1:T(8,128)(2,1)S(1)}, bf16[256,128]{0,1:T(8,128)(2,1)}, u32[]{:S(2)}) copy-start(bf16[256,128]{0,1:T(8,128)(2,1)} %reduce-scatter.3.cloned.1.call-done) | copy-start | bytes 196612
  827.8 5.7 copy-start.6
  827.8 5.7 copy-start.28
  827.8 5.8 copy-start.30
  827.8 5.7 copy-start.32
  827.8 5.7 copy-start.39
  827.8 5.7 copy-start.42
  827.8 5.7 copy-start.44
  827.8 5.7 copy-start.46
  833.6 1.6 copy-start.9
  1096.0 21.2 %copy-start.1 = (bf16[8,16,8192]{2,1,0:T(8,128)(2,1)S(1)}, bf16[8,16,8192]{2,1,0:T(8,128)(2,1)}, u32[]{:S(2)}) copy-start(bf16[8,16,8192]{2,1,0:T(8,128)(2,1)} %param.51) | copy-start | bytes 6291460
Sparse Core Ops, SparseCore 0:
  9.6 66.9 all-gather.5
  78.1 58.2 all-gather.7
  138.0 201.5 all-gather.9
  341.0 201.4 all-gather.11
  640.2 91.9 reduce-scatter.4
  735.9 62.1 reduce-scatter.2
  806.1 289.8 all-reduce.2
where the time goes:
time: 1130 us; the launch traced here: 1120 us
  waiting for transfers between devices  751 us (66%)
  matrix products  190 us (17%)
  blocking collectives  93.4 us (8%)
  local copies, waits for them, and re-layouts  42.9 us (4%)
  other arithmetic  25.7 us (2%)
  between operations  21.2 us (2%)
    psum x1, waiting for transfers between devices, body(): lax.psum((spread_table(onehot, query_first_grad), spread_table(onehot, qu...  259 us
    all_gather x1, waiting for transfers between devices, body(): lax.all_gather(shrink_weight, 'wt', axis=0, tiled=True)  170 us
    all_gather x1, waiting for transfers between devices, body(): lax.all_gather(expand_weight, 'wt', axis=0, tiled=True)  152 us
    dot_general x14, matrix products, matmul_right_t(): lax.dot_general(left, right, (((1,), (1,)), ((), ())), preferred_element_...  82.1 us
    dot_general x14, matrix products, matmul(): return jnp.dot(left, right, preferred_element_type=jnp.float32)  76.2 us
    reduce_scatter x1, waiting for transfers between devices, body(): lax.psum_scatter(grad_values.astype(jnp.bfloat16), 'ctx', scatter_dimensi...  74.1 us
    reduce_scatter x1, waiting for transfers between devices, body(): lax.psum_scatter((grad_keys * score_scale).astype(jnp.bfloat16), 'ctx', s...  65 us
    all_gather x1, blocking collectives, body(): lax.all_gather(values_own, 'ctx', axis=0, tiled=True)  37.9 us
  transfers between devices with their start and end apart: 7, of which 6 were waited for; matrix products, arithmetic and copies ran while one was open for 11% of the time, Pallas kernels for 0%

commit v1 on v0

--- a/solution.py
+++ b/solution.py
@@ -10,6 +10,28 @@
 KEY_BLOCK = 512
 EPSILON = 1e-05
 LOWEST = -1e30
+
+
+def in_order(blocks, dim):
+    blocks = jnp.moveaxis(blocks, 0, dim)
+    shape = blocks.shape
+    return blocks.reshape(*shape[:dim], shape[dim] * shape[dim + 1], *shape[dim + 2 :])
+
+
+def doubled(x, axis):
+    peers = lax.axis_size(axis)
+    parts = x[None]
+    for level in range(peers.bit_length() - 1):
+        bit = 1 << level
+        other = lax.ppermute(parts, axis, [(i, i ^ bit) for i in range(peers)])
+        both = jnp.stack([parts, other])
+        upper = lax.axis_index(axis) >> level & 1
+        parts = jnp.where(upper == 0, both, both[::-1]).reshape(-1, *x.shape)
+    return parts
+
+
+def collect(x, axis, dim):
+    return in_order(doubled(x, axis), dim)
 
 
 def matmul(left, right):
@@ -112,7 +134,7 @@
     first_low = normed_one.astype(jnp.bfloat16)
     attn_first = jnp.concatenate([own_query_first, own_key_first, own_value_first], 1)
     low_rank = matmul(first_low, attn_first).astype(jnp.bfloat16)
-    base = fold_rows(first_low, lax.all_gather(qkv_weight, "wt", axis=0, tiled=True))
+    base = fold_rows(first_low, collect(qkv_weight, "wt", 0))
     query = (
         (base[:, :model_width] + matmul(low_rank[:, :rank_width], own_query_second))
         .astype(jnp.bfloat16)

time: 1130 us -> 1200 us (1.062)
  waiting for transfers between devices: 751 us -> 796 us
  other arithmetic: 25.7 us -> 52.8 us
    ppermute x0 -> x2, waiting for transfers between devices: none -> 151 us  [doubled(): other = lax.ppermute(parts, axis, [(i, i ^ bit) for i in range(peers)])]
    all_gather x1, waiting for transfers between devices: 152 us -> 12.4 us  [body(): lax.all_gather(expand_weight, 'wt', axis=0, tiled=True)]
    psum x1, waiting for transfers between devices: 259 us -> 289 us  [body(): lax.psum((spread_table(onehot, query_first_grad), spread_table(onehot, qu...]
    another operation x0 -> x3, other arithmetic: none -> 16.5 us  [doubled(): both = jnp.stack([parts, other])]
    select_n x0 -> x1, other arithmetic: none -> 12.3 us  [doubled(): parts = jnp.where(upper == 0, both, both[::-1]).reshape(-1, *x.shape)]
  transfers between devices with their start and end apart: 7 -> 9, of which waited for: 6 -> 8; matrix products, arithmetic and copies ran while one was open for 11% -> 14% of each run, Pallas kernels for 0% -> 0%
where the time goes in v1:
time: 1200 us; the launch traced here: 1190 us
  waiting for transfers between devices  796 us (66%)
  matrix products  184 us (15%)
  blocking collectives  92.3 us (8%)
  other arithmetic  52.8 us (4%)
  local copies, waits for them, and re-layouts  42.7 us (4%)
  between operations  21.1 us (2%)
    psum x1, waiting for transfers between devices, body(): lax.psum((spread_table(onehot, query_first_grad), spread_table(onehot, qu...  289 us
    all_gather x1, waiting for transfers between devices, body(): lax.all_gather(shrink_weight, 'wt', axis=0, tiled=True)  170 us
    ppermute x2, waiting for transfers between devices, doubled(): other = lax.ppermute(parts, axis, [(i, i ^ bit) for i in range(peers)])  151 us
    dot_general x14, matrix products, matmul_right_t(): lax.dot_general(left, right, (((1,), (1,)), ((), ())), preferred_element_...  79.5 us
    dot_general x14, matrix products, matmul(): return jnp.dot(left, right, preferred_element_type=jnp.float32)  76.7 us
    reduce_scatter x1, waiting for transfers between devices, body(): lax.psum_scatter(grad_values.astype(jnp.bfloat16), 'ctx', scatter_dimensi...  70.9 us
    reduce_scatter x1, waiting for transfers between devices, body(): lax.psum_scatter((grad_keys * score_scale).astype(jnp.bfloat16), 'ctx', s...  65 us
    all_gather x1, blocking collectives, body(): lax.all_gather(values_own, 'ctx', axis=0, tiled=True)  37.9 us
  transfers between devices with their start and end apart: 9, of which 8 were waited for; matrix products, arithmetic and copies ran while one was open for 14% of the time, Pallas kernels for 0%

profile of v1, /device:TPU:0, one launch (start us, length us, event | category | flops | bytes accessed | tf_op | source)
XLA Modules:
  0.0 1194.5 jit_solution(16879716331603967330)
XLA Ops:
  10.0 4.5 collective-permute-done
  14.5 2.8 pad_maximum_fusion.1
  17.4 5.4 fusion.82
  22.8 3.2 collective-permute-start.1
  26.5 21.0 %all-gather = s32[1,2048]{1,0:T(1,128)S(1)} all-gather(s32[1,256]{1,0:T(1,128)S(1)} %copy-done.26), channel_id=2, replica_groups=mesh['ctx'=8,'wt'=4] {'ctx'}, dimensions={1}, use_global_device_ids=true | all-gather | bytes 9216 | tf_op jit(solution)/shard_map/all_gather | solution.py:153
  58.5 1.6 convolution_convert_fusion.6
  62.1 146.0 %collective-permute-done.1 = bf16[2,512,2304]{2,1,0:T(8,128)(2,1)} collective-permute-done((bf16[2,512,2304]{2,1,0:T(8,128)(2,1)}, bf16[2,512,2304]{2,1,0:T(8,128)(2,1)}, u32[]{:S(2)}, u32[]{:S(2)}) %collective-permute-start.1) | collective-permute-done | bytes 4718624 | tf_op jit(solution)/shard_map/ppermute | solution.py:26
  208.2 8.3 pad_maximum_fusion
  216.5 12.3 %reverse_select_fusion = bf16[2,2,512,2304]{3,2,1,0:T(8,128)(2,1)} fusion(bf16[2,2,512,2304]{3,2,1,0:T(8,128)(2,1)} %pad_maximum_fusion, pred[]{:T(512)S(6)} %eq.73), kind=kLoop, calls=%fused_computation.68 | loop fusion | flops 4718592 | bytes 18874368 | tf_op jit(solution)/shard_map/jit(_where)/select_n | solution.py:29
  228.8 6.4 fusion.118
  238.7 33.4 %all_gather.25 = bf16[2048,128]{1,0:T(8,128)(2,1)} all-gather(bf16[256,128]{1,0:T(8,128)(2,1)S(1)} %fusion.115), channel_id=1, replica_groups=mesh['ctx'=8,'wt'=4] {'ctx'}, dimensions={0}, use_global_device_ids=true | all-gather | bytes 589824 | tf_op jit(solution)/shard_map/all_gather | solution.py:151
  272.4 5.0 while.39
  273.0 2.3 fusion.277
  275.3 2.0 select_reduce_fusion.2
  278.5 37.9 %all_gather.26 = bf16[2048,128]{1,0:T(8,128)(2,1)} all-gather(bf16[256,128]{1,0:T(8,128)(2,1)S(1)} %fusion.116), channel_id=1, replica_groups=mesh['ctx'=8,'wt'=4] {'ctx'}, dimensions={0}, use_global_device_ids=true | all-gather | bytes 589824 | tf_op jit(solution)/shard_map/all_gather | solution.py:152
  318.0 6.2 while.40
  318.3 5.9 fusion.282
  324.2 2.5 copy.45
  328.2 6.5 fusion.85
  340.1 12.4 %all-gather.8.cloned.1.call-done = bf16[2048,8192]{1,0:T(8,128)(2,1)} async-done(((bf16[512,8192]{1,0:T(8,128)(2,1)}), bf16[2048,8192]{1,0:T(8,128)(2,1)}) %all-gather.8.cloned.1.call-update) | async-done | bytes 33554448 | tf_op jit(solution)/shard_map/all_gather | solution.py:212
  352.6 22.3 %fusion.201 = f32[256,8192]{1,0:T(8,128)} fusion(bf16[256,2048]{1,0:T(8,128)(2,1)} %copy-done.19, bf16[2048,8192]{1,0:T(8,128)(2,1)} %all-gather.8.cloned.1.call-done), kind=kOutput, calls=%fused_computation.281 | convolution fusion | flops 8589934592 | bytes 42991616 | tf_op jit(solution)/shard_map/dot_general | solution.py:38
  374.9 10.4 multiply_convert_fusion
  385.3 170.4 %all-gather.10.cloned.1.call-done = bf16[8192,2048]{1,0:T(8,128)(2,1)} async-done(((bf16[2048,2048]{1,0:T(8,128)(2,1)}), bf16[8192,2048]{1,0:T(8,128)(2,1)}) %all-gather.10.cloned.1.call-update) | async-done | bytes 33554448 | tf_op jit(solution)/shard_map/all_gather | solution.py:217
  555.7 18.5 %fusion.124 = f32[256,8192]{1,0:T(8,128)} fusion(bf16[8192,2048]{1,0:T(8,128)(2,1)} %all-gather.10.cloned.1.call-done, bf16[1,256,2048]{2,1,0:T(8,128)(2,1)} %param.31), kind=kOutput, calls=%fused_computation.165 | convolution fusion | flops 8589934592 | bytes 42991616 | tf_op jit(solution)/shard_map/dot_general | solution.py:42
  574.2 23.2 %fusion.73 = bf16[256,8192]{1,0:T(8,128)(2,1)S(1)} fusion(f32[256,8192]{1,0:T(8,128)} %get-tuple-element.441, f32[256,8192]{1,0:T(8,128)} %fusion.124, bf16[16,256]{1,0:T(8,128)(2,1)S(1)} %convolution_convert_fusion.6, bf16[8,8192,16]{1,2,0:T(8,128)(2,1)} %param.52, s32[]{:T(128)S(6)} %select_n.102), kind=kOutput, calls=%fused_computation.79 | convolution fusion | flops 115343360 | bytes 21241860 | tf_op jit(solution)/shard_map/dot_general | solution.py:42
  597.4 2.0 copy-done.13
  600.6 17.0 %fusion.202 = f32[256,2048]{1,0:T(8,128)} fusion(bf16[256,8192]{1,0:T(8,128)(2,1)} %copy-done.13, bf16[2048,8192]{1,0:T(8,128)(2,1)} %all-gather.8.cloned.1.call-done), kind=kOutput, calls=%fused_computation.282 | convolution fusion | flops 8589934592 | bytes 39845888 | tf_op jit(solution)/shard_map/dot_general | solution.py:42
  617.6 2.6 fusion.198
  621.1 2.3 convolution_convert_fusion.5
  623.4 2.4 fusion.195
  630.4 15.0 %while.41 = (s32[]{:T(128)}, f32[256,16,128]{2,0,1:T(8,128)S(1)}, f32[2048,128]{0,1:T(8,128)}, bf16[2048,128]{0,1:T(8,128)(2,1)}, s32[]{:T(128)}, /*index=5*/s32...) while((s32[]{:T(128)}, f32[256,16,128]{2,0,1:T(8,128)S(1)}, ...), condition=%wide.region_15.16_spmd.clone, body=%wide.region_14.15_spmd.clone.sunk | while | flops 2710438656 | bytes 55899472 | solution.py:273
  630.5 2.2 fusion.293
  633.0 4.1 fusion.294
  637.1 2.6 convolution_add_fusion.13
  639.7 2.3 fusion.295
  642.0 2.5 fusion.296
  645.5 2.1 multiply_convert_fusion.2
  648.3 1.9 copy.49
  650.2 2.0 multiply_convert_fusion.1
  653.4 1.6 fusion.205
  655.8 2.3 convolution_convert_fusion.9
  659.9 1.8 broadcast_multiply_fusion.2
  661.7 2.6 broadcast_multiply_fusion.1
  664.3 2.4 broadcast_multiply_fusion
  666.7 70.9 %reduce-scatter.5.cloned.1.call-done = bf16[256,128]{0,1:T(8,128)(2,1)} async-done(((bf16[2048,128]{0,1:T(8,128)(2,1)}), bf16[256,128]{0,1:T(8,128)(2,1)}) %reduce-scatter.5.cloned.1.call-update) | async-done | bytes 65552 | tf_op jit(solution)/shard_map/reduce_scatter | solution.py:280
  738.6 65.0 %reduce-scatter.3.cloned.1.call-done = bf16[256,128]{0,1:T(8,128)(2,1)} async-done(((bf16[2048,128]{0,1:T(8,128)(2,1)}), bf16[256,128]{0,1:T(8,128)(2,1)}) %reduce-scatter.3.cloned.1.call-update) | async-done | bytes 65552 | tf_op jit(solution)/shard_map/reduce_scatter | solution.py:277
  807.6 2.6 broadcast_multiply_fusion.3
  810.2 1.9 copy-done.4
  812.0 18.5 %convolution_add_fusion.9 = f32[256,2048]{1,0:T(8,128)S(1)} fusion(f32[256,2048]{1,0:T(8,128)S(1)} %copy-done.4, bf16[256,8192]{1,0:T(8,128)(2,1)} %get-tuple-element.440, bf16[8192,2048]{1,0:T(8,128)(2,1)} %all-gather.10.cloned.1.call-done), kind=kOutput, calls=%fused_computation.105 | convolution fusion | flops 8590458880 | bytes 41943040 | tf_op jit(solution)/shard_map/dot_general | solution.py:38
  830.6 2.3 fusion.95
  832.9 35.3 %all-gather.12.cloned.1.call-done = bf16[2048,2304]{1,0:T(8,128)(2,1)} async-done(((bf16[512,2304]{1,0:T(8,128)(2,1)}), bf16[2048,2304]{1,0:T(8,128)(2,1)}) %all-gather.12.cloned.1.call-update) | async-done | bytes 9437200 | tf_op jit(solution)/shard_map/all_gather | solution.py:297
  868.2 5.2 fusion.109
  875.1 1.7 fusion.120
  876.8 289.2 %all-reduce.3.cloned.1.call-done = (f32[8,2048,16]{1,2,0:T(8,128)}, f32[8,16,2048]{2,1,0:T(8,128)}, f32[8,2048,16]{1,2,0:T(8,128)}, f32[8,16,128]{2,1,0:T(8,128)...) async-done(((f32[8,2048,16]{1,2,0:T(8,128)}, ...) | async-done | bytes 16908304 | tf_op jit(solution)/shard_map/psum | solution.py:310
  1166.1 1.8 constant_dynamic-slice_fusion.11
  1167.9 1.7 constant_dynamic-slice_fusion.10
  1169.6 1.7 constant_dynamic-slice_fusion.9
  1171.2 1.7 constant_dynamic-slice_fusion.7
  1176.0 1.7 constant_dynamic-slice_fusion.5
  1177.7 1.7 constant_dynamic-slice_fusion.4
  1179.3 1.7 constant_dynamic-slice_fusion.3
  1181.0 2.3 constant_dynamic-slice_fusion.2
  1183.3 2.3 constant_dynamic-slice_fusion.1
  1185.6 1.7 constant_dynamic-slice_fusion
  (192 shorter events, 46.2 us)
Async XLA Ops:
  7.2 367.7 %copy-start = (bf16[8,16,8192]{2,1,0:T(8,128)(2,1)S(1)}, bf16[8,16,8192]{2,1,0:T(8,128)(2,1)}, u32[]{:S(2)}) copy-start(bf16[8,16,8192]{2,1,0:T(8,128)(2,1)} %param.51) | copy-start | bytes 6291460
  7.2 321.0 %all-gather.6.cloned.1.call-start = ((), (), s32[]{:S(2)}) async-start(), calls=%async_computation.2 | async-start | bytes 10485760 | tf_op jit(solution)/shard_map/all_gather | solution.py:206
  7.9 344.7 %all-gather.8.cloned.1.call-start = ((), (), s32[]{:S(2)}) async-start(), calls=%async_computation.3 | async-start | bytes 41943040 | tf_op jit(solution)/shard_map/all_gather | solution.py:212
  8.7 547.0 %all-gather.10.cloned.1.call-start = ((), (), s32[]{:S(2)}) async-start(), calls=%async_computation.4 | async-start | bytes 41943040 | tf_op jit(solution)/shard_map/all_gather | solution.py:217
  9.4 728.2 %reduce-scatter.5.cloned.1.call-start = ((), (), s32[]{:S(2)}) async-start(), calls=%async_computation.6 | async-start | bytes 589824 | tf_op jit(solution)/shard_map/reduce_scatter | solution.py:280
  9.5 5.1 collective-permute-start
  17.3 8.7 copy-start.26
  17.3 37.9 %copy-start.5 = (bf16[1,256,2048]{2,1,0:T(8,128)(2,1)S(1)}, bf16[1,256,2048]{2,1,0:T(8,128)(2,1)}, u32[]{:S(2)}) copy-start(bf16[1,256,2048]{2,1,0:T(8,128)(2,1)} %param.30) | copy-start | bytes 3145732
  22.8 37.4 %copy-start.40 = (f32[2048]{0:T(1024)S(1)}, f32[2048]{0:T(1024)}, u32[]{:S(2)}) copy-start(f32[2048]{0:T(1024)} %param.34) | copy-start | bytes 24580
  22.8 37.4 %copy-start.48 = (f32[2048]{0:T(1024)S(1)}, f32[2048]{0:T(1024)}, u32[]{:S(2)}) copy-start(f32[2048]{0:T(1024)} %param.35) | copy-start | bytes 24580
  22.8 185.4 %collective-permute-start.1 = (bf16[2,512,2304]{2,1,0:T(8,128)(2,1)}, bf16[2,512,2304]{2,1,0:T(8,128)(2,1)}, u32[]{:S(2)}, u32[]{:S(2)}) collective-permute-start(bf16[2,512,2304]{2,1,0:T(8,128)(2,1)} %get-tuple-element.424), channel_id=1, source_target_pairs={{0,2},{1,3},{2,0},{3,1},{4,6},{5,7},{6,4},{7,5},{8,10},{9,11},{10,... | collective-permute-start | bytes 14155784 | tf_op jit(solution)/shard_map/ppermute | solution.py:26
  55.5 173.3 %copy-start.44 = (f32[256]{0:T(256)}, f32[256]{0:T(256)S(1)}, u32[]{:S(2)}) copy-start(f32[256]{0:T(256)S(1)} %broadcast_multiply_fusion.17) | copy-start | bytes 3076
  55.9 172.8 %copy-start.46 = (f32[256]{0:T(256)}, f32[256]{0:T(256)S(1)}, u32[]{:S(2)}) copy-start(f32[256]{0:T(256)S(1)} %add_rsqrt_fusion.1) | copy-start | bytes 3076
  56.8 159.7 %copy-start.27 = (bf16[2048,16]{0,1:T(8,128)(2,1)}, bf16[2048,16]{0,1:T(8,128)(2,1)S(1)}, u32[]{:S(2)}) copy-start(bf16[2048,16]{0,1:T(8,128)(2,1)S(1)} %dynamic-slice_bitcast_fusion.2) | copy-start | bytes 196612
  57.7 4.4 copy-start.31
  57.7 158.8 %copy-start.29 = (bf16[2048,16]{0,1:T(8,128)(2,1)}, bf16[2048,16]{0,1:T(8,128)(2,1)S(1)}, u32[]{:S(2)}) copy-start(bf16[2048,16]{0,1:T(8,128)(2,1)S(1)} %get-tuple-element.444) | copy-start | bytes 196612
  60.7 1.0 copy-start.20
  62.1 215.3 %copy-start.35 = (bf16[256,48]{0,1:T(8,128)(2,1)}, bf16[256,48]{0,1:T(8,128)(2,1)S(1)}, u32[]{:S(2)}) copy-start(bf16[256,48]{0,1:T(8,128)(2,1)S(1)} %convolution_convert_fusion) | copy-start | bytes 73732
  235.2 37.2 %copy-start.22 = (f32[256,2304]{1,0:T(8,128)}, f32[256,2304]{1,0:T(8,128)S(1)}, u32[]{:S(2)}) copy-start(f32[256,2304]{1,0:T(8,128)S(1)} %fusion.118) | copy-start | bytes 7077892
  328.2 6.5 copy-start.37
  334.7 2.8 copy-start.39
  334.7 2.8 copy-start.49
  336.1 1.4 copy-start.2
  338.0 1.0 copy-start.19
  340.1 34.7 %copy-start.42 = (bf16[256,16]{0,1:T(8,128)(2,1)}, bf16[256,16]{0,1:T(8,128)(2,1)S(1)}, u32[]{:S(2)}) copy-start(bf16[256,16]{0,1:T(8,128)(2,1)S(1)} %convolution_convert_fusion.7) | copy-start | bytes 24580
  597.4 2.0 copy-start.13
  600.6 17.0 %copy-start.3 = (f32[256,2048]{1,0:T(8,128)S(1)}, f32[256,2048]{1,0:T(8,128)}, u32[]{:S(2)}) copy-start(f32[256,2048]{1,0:T(8,128)} %copy-done.2) | copy-start | bytes 6291460
  617.6 2.6 copy-start.15
  617.6 5.7 slice-start
  620.2 3.1 slice-start.1
  621.0 4.7 copy-start.7
  625.8 2.7 copy-start.11
  630.4 2.6 copy-start.25
  639.7 2.3 copy-start.23
  644.5 0.8 copy-start.24
  645.5 158.0 %reduce-scatter.3.cloned.1.call-start = ((), (), s32[]{:S(2)}) async-start(), calls=%async_computation.5 | async-start | bytes 589824 | tf_op jit(solution)/shard_map/reduce_scatter | solution.py:277
  647.7 220.5 %all-gather.12.cloned.1.call-start = ((), (), s32[]{:S(2)}) async-start(), calls=%async_computation.7 | async-start | bytes 11796480 | tf_op jit(solution)/shard_map/all_gather | solution.py:297
  648.3 517.8 %all-reduce.3.cloned.1.call-start = ((), (), s32[]{:S(2)}) async-start(), calls=%async_computation.8 | async-start | bytes 33816576 | tf_op jit(solution)/shard_map/psum | solution.py:310
  648.3 6.6 copy-start.10
  650.2 5.1 copy-start.36
  650.2 5.5 copy-start.12
  652.2 3.1 copy-start.17
  653.4 4.7 copy-start.16
  654.9 3.4 copy-start.8
  655.0 3.4 copy-start.38
  655.7 2.8 copy-start.14
  655.7 2.8 copy-start.43
  661.7 145.5 %copy-start.21 = (bf16[256,2048]{1,0:T(8,128)(2,1)S(1)}, bf16[256,2048]{1,0:T(8,128)(2,1)}, u32[]{:S(2)}) copy-start(bf16[256,2048]{1,0:T(8,128)(2,1)} %copy-done.20) | copy-start | bytes 3145732
  810.1 1.9 copy-start.4
  812.0 56.2 %copy-start.18 = (bf16[256,16,128]{0,2,1:T(8,128)(2,1)S(1)}, bf16[256,16,128]{0,2,1:T(8,128)(2,1)}, u32[]{:S(2)}) copy-start(bf16[256,16,128]{0,2,1:T(8,128)(2,1)} %copy-done.17) | copy-start | bytes 3145732
  812.0 56.2 %copy-start.33 = (bf16[256,128]{0,1:T(8,128)(2,1)S(1)}, bf16[256,128]{0,1:T(8,128)(2,1)}, u32[]{:S(2)}) copy-start(bf16[256,128]{0,1:T(8,128)(2,1)} %reduce-scatter.5.cloned.1.call-done) | copy-start | bytes 196612
  812.0 56.2 %copy-start.34 = (bf16[256,128]{0,1:T(8,128)(2,1)S(1)}, bf16[256,128]{0,1:T(8,128)(2,1)}, u32[]{:S(2)}) copy-start(bf16[256,128]{0,1:T(8,128)(2,1)} %reduce-scatter.3.cloned.1.call-done) | copy-start | bytes 196612
  832.8 40.6 %copy-start.6 = (bf16[1,256,2048]{2,1,0:T(8,128)(2,1)S(1)}, bf16[1,256,2048]{2,1,0:T(8,128)(2,1)}, u32[]{:S(2)}) copy-start(bf16[1,256,2048]{2,1,0:T(8,128)(2,1)} %param.30) | copy-start | bytes 3145732
  832.8 40.6 %copy-start.28 = (bf16[2048,16]{0,1:T(8,128)(2,1)S(1)}, bf16[2048,16]{0,1:T(8,128)(2,1)}, u32[]{:S(2)}) copy-start(bf16[2048,16]{0,1:T(8,128)(2,1)} %copy-done.27) | copy-start | bytes 196612
  832.8 40.6 %copy-start.30 = (bf16[2048,16]{0,1:T(8,128)(2,1)S(1)}, bf16[2048,16]{0,1:T(8,128)(2,1)}, u32[]{:S(2)}) copy-start(bf16[2048,16]{0,1:T(8,128)(2,1)} %copy-done.29) | copy-start | bytes 196612
  832.8 40.6 %copy-start.32 = (bf16[2048,16]{0,1:T(8,128)(2,1)S(1)}, bf16[2048,16]{0,1:T(8,128)(2,1)}, u32[]{:S(2)}) copy-start(bf16[2048,16]{0,1:T(8,128)(2,1)} %copy-done.31) | copy-start | bytes 196612
  832.8 40.6 %copy-start.41 = (f32[2048]{0:T(1024)S(1)}, f32[2048]{0:T(1024)}, u32[]{:S(2)}) copy-start(f32[2048]{0:T(1024)} %param.34) | copy-start | bytes 24580
  832.9 40.6 %copy-start.45 = (f32[256]{0:T(256)S(1)}, f32[256]{0:T(256)}, u32[]{:S(2)}) copy-start(f32[256]{0:T(256)} %copy-done.44) | copy-start | bytes 3076
  832.9 40.6 %copy-start.47 = (f32[256]{0:T(256)S(1)}, f32[256]{0:T(256)}, u32[]{:S(2)}) copy-start(f32[256]{0:T(256)} %copy-done.46) | copy-start | bytes 3076
  873.5 1.6 copy-start.9
  1166.1 21.2 %copy-start.1 = (bf16[8,16,8192]{2,1,0:T(8,128)(2,1)S(1)}, bf16[8,16,8192]{2,1,0:T(8,128)(2,1)}, u32[]{:S(2)}) copy-start(bf16[8,16,8192]{2,1,0:T(8,128)(2,1)} %param.51) | copy-start | bytes 6291460
Sparse Core Ops, SparseCore 0:
  9.6 102.6 all-gather.5
  113.8 238.7 all-gather.7
  354.2 201.4 all-gather.9
  645.6 91.9 reduce-scatter.4
  741.3 62.1 reduce-scatter.2
  804.9 63.1 all-gather.11
  875.2 290.8 all-reduce.2
